TPU v7x, 32 devices: a whole 2x2x4 slice. The times are simulated.
32 devices in a mesh: dp: 2 (over x), fsdp: 4 (over z), tensor: 4 (over y, core).
Axes of the slice: x: 2, y: 2, z: 4, core: 2. Of those that a mesh axis runs over, the one named last changes fastest.
Arguments:
- grads: bfloat16 [2, 4, 16, 53248], P('dp', 'fsdp', None, 'tensor'), may hold values from -64 to 64, as said below
- params: bfloat16 [16, 53248], P('fsdp', 'tensor'), may hold values from -0.119628906 to 0.119628906
- moment_norm: bfloat16 [16, 53248], P('fsdp', 'tensor'), may hold values from -1 to 1
- moment_scale: float32 [16, 416], P('fsdp', 'tensor'), may hold values from 0.05 to 0.5
- second_norm: bfloat16 [16, 53248], P('fsdp', 'tensor'), may hold values from 0.049804688 to 1
- second_rows: float32 [16], P('fsdp'), may hold values from 0.01 to 0.1
- second_cols: float32 [53248], P('tensor'), may hold values from 0.01 to 0.1
Outputs:
- new_params: bfloat16 [16, 53248], P(None, 'tensor')
- next_moment: bfloat16 [16, 53248], P('fsdp', 'tensor')
- next_moment_scale: float32 [16, 416], P('fsdp', 'tensor')
- next_second: bfloat16 [16, 53248], P('fsdp', 'tensor')
- next_second_rows: float32 [16], P('fsdp')
- next_second_cols: float32 [53248], P('tensor')
Inputs may be any that keep to these rules, and one draw needn't show every extreme that they name: `grads`: partial gradients; magnitudes are at most 64.
All inputs are finite; a program needn't handle non-finite values. Where the computation divides by a largest or mean magnitude, that divisor is 1e-20 or more.
Results may differ from a plain program's by a relative error of at most 0.0004.
Values may be sent and summed in bfloat16 or wider, within the bound.
No kernel may reach another device: no remote copies, remote signals or barrier semaphores. Data moves between devices by JAX's collectives and lax.ppermute only.
A program may use at most 64 MiB of HBM per device.

v0:
```python
import math
import jax
import jax.numpy as jnp
from jax import lax
from jax.sharding import PartitionSpec as P

BLOCK = 128
STEP = 10
beta_one = 0.9
beta_two = 0.95
learn_rate = 0.01
decay_weight = 0.1
clip_rms = 0.3


def on_device(grads, params, moment_norm, moment_scale, second_norm, second_rows, second_cols):
    local = grads[0, 0].astype(jnp.float32)
    replicas = lax.psum(local, "dp")
    summed = lax.psum_scatter(replicas, "fsdp", scatter_dimension=0, tiled=True)
    own_rows, own_cols = summed.shape
    fsdp_count = lax.axis_size("fsdp")
    tensor_count = lax.axis_size("tensor")
    limit = clip_rms * math.sqrt(own_rows * fsdp_count * own_cols * tensor_count)
    total = lax.psum(jnp.sum(summed * summed), ("fsdp", "tensor"))
    factor = jnp.minimum(jnp.float32(1.0), limit / jnp.sqrt(total + 1e-06))
    clipped = factor * summed
    blocks = own_cols // BLOCK
    first_old = (
        moment_norm.astype(jnp.float32).reshape(own_rows, blocks, BLOCK) * moment_scale[:, :, None]
    ).reshape(own_rows, own_cols)
    first = beta_one * first_old + (1.0 - beta_one) * clipped
    second_old = second_norm.astype(jnp.float32) * jnp.minimum(
        second_rows[:, None], second_cols[None, :]
    )
    second = beta_two * second_old + (1.0 - beta_two) * clipped * clipped
    plain = params.astype(jnp.float32)
    ratio = first / (1.0 - beta_one**STEP) / (jnp.sqrt(second / (1.0 - beta_two**STEP)) + 1e-08)
    updated = (plain - learn_rate * (ratio + decay_weight * plain)).astype(jnp.bfloat16)
    new_params = lax.all_gather(updated, "fsdp", axis=0, tiled=True)
    grouped = first.reshape(own_rows, blocks, BLOCK)
    next_moment_scale = jnp.max(jnp.abs(grouped), axis=2)
    next_moment = (
        (grouped / (next_moment_scale[:, :, None] + 1e-06))
        .reshape(own_rows, own_cols)
        .astype(jnp.bfloat16)
    )
    row_local = jnp.max(second, axis=1)
    col_local = jnp.max(second, axis=0)
    row_peak = lax.pmax(row_local, "tensor")
    col_peak = lax.pmax(col_local, "fsdp")
    next_second = (second / jnp.minimum(row_peak[:, None], col_peak[None, :])).astype(jnp.bfloat16)
    return (new_params, next_moment, next_moment_scale, next_second, row_peak, col_peak)


def solution(mesh):
    in_specs = (
        P("dp", "fsdp", None, "tensor"),
        P("fsdp", "tensor"),
        P("fsdp", "tensor"),
        P("fsdp", "tensor"),
        P("fsdp", "tensor"),
        P("fsdp"),
        P("tensor"),
    )
    out_specs = (
        P(None, "tensor"),
        P("fsdp", "tensor"),
        P("fsdp", "tensor"),
        P("fsdp", "tensor"),
        P("fsdp"),
        P("tensor"),
    )
    return jax.shard_map(
        on_device, mesh=mesh, in_specs=in_specs, out_specs=out_specs, check_vma=False
    )
```

profile of v0, /device:TPU:0, one launch (start us, length us, event | category | flops | bytes accessed | tf_op | source)
XLA Modules:
  0.0 167.2 jit_solution(14253228319640697311)
XLA Ops:
  7.2 0.0 copy-start
  7.2 0.0 all-reduce.6.cloned.1.call-start
  7.2 2.0 %bitcast_convert_fusion = f32[16,13312]{1,0:T(8,128)} fusion(bf16[1,1,16,13312]{3,2,1,0:T(8,128)(2,1)} %param.7), kind=kLoop, calls=%fused_computation | loop fusion | flops 212992 | bytes 1277952 | tf_op jit(solution)/shard_map/convert_element_type | solution.py:17
  9.2 0.0 all-reduce.6.cloned.1.call-update
  9.2 0.0 all-reduce.4.cloned.1.call-start
  9.3 0.0 copy-start.10
  9.3 0.6 copy-done.10
  10.0 0.6 dynamic-slice
  11.2 47.7 %all-reduce.6.cloned.1.call-done = f32[16,13312]{1,0:T(8,128)} async-done(((f32[16,13312]{1,0:T(8,128)}), f32[16,13312]{1,0:T(8,128)}) %all-reduce.6.cloned.1.call-update) | async-done | bytes 851984
  58.9 1.7 %constant_dynamic-slice_fusion = f32[4,13312]{1,0:T(4,128)} fusion(f32[16,13312]{1,0:T(8,128)} %all-reduce.6.cloned.1.call-done, u32[]{:T(128)S(6)} %multiply.4), kind=kLoop, calls=%fused_computation.22 | loop fusion | bytes 425988
  60.6 0.0 copy-start.6
  60.6 0.0 all-reduce.4.cloned.1.call-update
  60.6 22.8 %all-reduce.4.cloned.1.call-done = f32[4,13312]{1,0:T(4,128)} async-done(((f32[4,13312]{1,0:T(4,128)}), f32[4,13312]{1,0:T(4,128)}) %all-reduce.4.cloned.1.call-update) | async-done | bytes 213008 | tf_op jit(solution)/shard_map/psum | solution.py:18
  83.4 0.0 copy-start.1
  83.4 1.7 %multiply_reduce_fusion = f32[]{:T(128)} fusion(f32[4,13312]{1,0:T(4,128)} %all-reduce.4.cloned.1.call-done), kind=kLoop, calls=%fused_computation.15 | loop fusion | flops 106495 | bytes 212996 | tf_op jit(solution)/shard_map/reduce_sum | solution.py:24
  85.2 0.0 copy-done
  85.2 0.0 copy-start.3
  85.2 0.0 copy-start.4
  85.2 0.1 broadcast_bitcast_fusion.1
  85.3 33.3 %psum.15 = f32[]{:T(128)} all-reduce(f32[]{:T(128)} %multiply_reduce_fusion), channel_id=1, replica_groups=mesh['dp'=2,'fsdp'=4,'tensor'=4] {'fsdp','tensor'}, use_global_device_ids=true, to_apply=%region_3.0 | all-reduce | flops 1 | bytes 8 | tf_op jit(solution)/shard_map/psum | solution.py:24
  119.3 0.0 copy-start.8
  119.3 0.0 copy-done.6
  119.3 0.0 copy-done.1
  119.3 0.0 copy-done.3
  119.3 0.0 copy-done.4
  119.3 0.6 copy-done.8
  119.9 0.5 abs_bitcast_fusion
  120.4 0.1 bitcast_reduce_fusion
  120.5 0.0 copy-start.7
  120.6 0.1 broadcast_bitcast_fusion
  120.7 0.4 copy-done.7
  121.1 0.0 copy-start.5
  121.1 16.5 %pmax.15 = f32[13312]{0:T(1024)S(1)} all-reduce(f32[13312]{0:T(1024)S(1)} %get-tuple-element.14), channel_id=1, replica_groups=mesh['dp'=2,'fsdp'=4,'tensor'=4] {'fsdp'}, use_global_device_ids=true, to_apply=%region_8.0 | all-reduce | flops 13312 | bytes 106496 | tf_op jit(solution)/shard_map/pmax | solution.py:50
  137.6 0.0 copy-start.2
  137.6 5.8 %pmax.14 = f32[4]{0:T(128)S(1)} all-reduce(f32[4]{0:T(128)S(1)} %get-tuple-element.15), channel_id=1, replica_groups=mesh['dp'=2,'fsdp'=4,'tensor'=4] {'tensor'}, use_global_device_ids=true, to_apply=%region_6.0 | all-reduce | flops 4 | bytes 32 | tf_op jit(solution)/shard_map/pmax | solution.py:49
  143.4 0.0 copy-start.9
  143.4 0.5 copy-done.9
  143.9 0.0 copy-done.5
  143.9 1.0 fusion.6
  144.9 0.0 copy-done.2
  144.9 14.6 %all-gather = bf16[4,4,13312]{2,1,0:T(4,128)(2,1)S(1)} all-gather(bf16[1,4,13312]{2,1,0:T(4,128)(2,1)S(1)} %get-tuple-element.12), channel_id=1, replica_groups=mesh['dp'=2,'fsdp'=4,'tensor'=4] {'fsdp'}, dimensions={0}, use_global_device_ids=true | all-gather | bytes 532480 | tf_op jit(solution)/shard_map/all_gather | solution.py:39
  159.5 0.9 reshape.32
  (1 shorter events, 0.0 us)
Async XLA Ops:
  7.2 78.0 %copy-start = (f32[4,104]{1,0:T(4,128)S(1)}, f32[4,104]{1,0:T(4,128)}, u32[]{:S(2)}) copy-start(f32[4,104]{1,0:T(4,128)} %param.10) | copy-start | bytes 4996
  7.2 51.7 %all-reduce.6.cloned.1.call-start = ((), (), s32[]{:S(2)}) async-start(), calls=%async_computation.1 | async-start | bytes 1703936
  9.2 74.2 %all-reduce.4.cloned.1.call-start = ((), (), s32[]{:S(2)}) async-start(), calls=%async_computation | async-start | bytes 425984 | tf_op jit(solution)/shard_map/psum | solution.py:18
  9.3 0.7 copy-start.10
  60.6 58.7 %copy-start.6 = (f32[13312]{0:T(1024)S(1)}, f32[13312]{0:T(1024)}, u32[]{:S(2)}) copy-start(f32[13312]{0:T(1024)} %param.13) | copy-start | bytes 159748
  83.4 35.9 %copy-start.1 = (f32[4,13312]{1,0:T(4,128)S(1)}, f32[4,13312]{1,0:T(4,128)}, u32[]{:S(2)}) copy-start(f32[4,13312]{1,0:T(4,128)} %all-reduce.4.cloned.1.call-done) | copy-start | bytes 638980
  85.2 34.1 %copy-start.3 = (bf16[4,13312]{1,0:T(4,128)(2,1)S(1)}, bf16[4,13312]{1,0:T(4,128)(2,1)}, u32[]{:S(2)}) copy-start(bf16[4,13312]{1,0:T(4,128)(2,1)} %param.9) | copy-start | bytes 319492
  85.2 34.1 %copy-start.4 = (bf16[4,13312]{1,0:T(4,128)(2,1)S(1)}, bf16[4,13312]{1,0:T(4,128)(2,1)}, u32[]{:S(2)}) copy-start(bf16[4,13312]{1,0:T(4,128)(2,1)} %param.11) | copy-start | bytes 319492
  119.3 0.7 copy-start.8
  120.5 0.6 copy-start.7
  121.1 22.8 %copy-start.5 = (bf16[4,13312]{1,0:T(4,128)(2,1)S(1)}, bf16[4,13312]{1,0:T(4,128)(2,1)}, u32[]{:S(2)}) copy-start(bf16[4,13312]{1,0:T(4,128)(2,1)} %param.8) | copy-start | bytes 319492
  137.6 7.3 %copy-start.2 = (f32[13312]{0:T(1024)}, f32[13312]{0:T(1024)S(1)}, u32[]{:S(2)}) copy-start(f32[13312]{0:T(1024)S(1)} %pmax.15) | copy-start | bytes 159748
  143.4 0.5 copy-start.9
Sparse Core Ops, SparseCore 0:
  10.4 48.4 all-reduce.5
  61.7 21.6 all-reduce.3
where the time goes:
time: 168 us; the launch traced here: 167 us
  waiting for transfers between devices  70.5 us (42%)
  blocking collectives  70.1 us (42%)
  between operations  15.5 us (9%)
  local copies, waits for them, and re-layouts  5.64 us (3%)
  other arithmetic  5.35 us (3%)
    unnamed x3, waiting for transfers between devices  47.7 us
    psum x1, blocking collectives, on_device(): total = lax.psum(jnp.sum(summed * summed), ('fsdp', 'tensor'))  33.3 us
    psum x1, waiting for transfers between devices, on_device(): replicas = lax.psum(local, 'dp')  22.8 us
    pmax x1, blocking collectives, on_device(): col_peak = lax.pmax(col_local, 'fsdp')  16.5 us
    all_gather x1, blocking collectives, on_device(): new_params = lax.all_gather(updated, 'fsdp', axis=0, tiled=True)  14.6 us
    pmax x1, blocking collectives, on_device(): row_peak = lax.pmax(row_local, 'tensor')  5.76 us
    unnamed x27, local copies, waits for them, and re-layouts  5.64 us
  transfers between devices with their start and end apart: 2, of which 2 were waited for; matrix products, arithmetic and copies ran while one was open for 0% of the time, Pallas kernels for 0%

commit v1 on v0

--- a/solution.py
+++ b/solution.py
@@ -13,9 +13,13 @@
 clip_rms = 0.3
 
 
+def prepare_the_heads(array_in):
+    return array_in + lax.ppermute(array_in, "dp", [(0, 1), (1, 0)])
+
+
 def on_device(grads, params, moment_norm, moment_scale, second_norm, second_rows, second_cols):
     local = grads[0, 0].astype(jnp.float32)
-    replicas = lax.psum(local, "dp")
+    replicas = prepare_the_heads(local)
     summed = lax.psum_scatter(replicas, "fsdp", scatter_dimension=0, tiled=True)
     own_rows, own_cols = summed.shape
     fsdp_count = lax.axis_size("fsdp")

time: 168 us -> 162 us (0.964)
  waiting for transfers between devices: 70.5 us -> 64.5 us
  starting transfers between devices: 0.08 us -> 3.07 us
  local copies, waits for them, and re-layouts: 5.64 us -> 3.93 us
  blocking collectives: 70.1 us -> 68.4 us
    psum x1 -> x0, waiting for transfers between devices: 22.8 us -> none  [on_device(): replicas = lax.psum(local, 'dp')]
    ppermute x0 -> x1, waiting for transfers between devices: none -> 18.9 us  [prepare_the_heads(): return array_in + lax.ppermute(array_in, 'dp', [(0, 1), (1, 0)])]
    ppermute x0 -> x1, starting transfers between devices: none -> 3.03 us  [prepare_the_heads(): return array_in + lax.ppermute(array_in, 'dp', [(0, 1), (1, 0)])]
    unnamed x3 -> x2, waiting for transfers between devices: 47.7 us -> 45.5 us
    unnamed x27 -> x26, local copies, waits for them, and re-layouts: 5.64 us -> 3.93 us
where the time goes in v1:
time: 162 us
  blocking collectives  68.4 us (42%)
  waiting for transfers between devices  64.5 us (40%)
  between operations  15.5 us (10%)
  other arithmetic  6.52 us (4%)
  local copies, waits for them, and re-layouts  3.93 us (2%)
  starting transfers between devices  3.07 us (2%)
    unnamed x2, waiting for transfers between devices  45.5 us
    psum x1, blocking collectives, on_device(): total = lax.psum(jnp.sum(summed * summed), ('fsdp', 'tensor'))  31.7 us
    ppermute x1, waiting for transfers between devices, prepare_the_heads(): return array_in + lax.ppermute(array_in, 'dp', [(0, 1), (1, 0)])  18.9 us
    pmax x1, blocking collectives, on_device(): col_peak = lax.pmax(col_local, 'fsdp')  16.5 us
    all_gather x1, blocking collectives, on_device(): new_params = lax.all_gather(updated, 'fsdp', axis=0, tiled=True)  14.6 us
    pmax x1, blocking collectives, on_device(): row_peak = lax.pmax(row_local, 'tensor')  5.76 us
    unnamed x26, local copies, waits for them, and re-layouts  3.93 us
  transfers between devices with their start and end apart: 2, of which 2 were waited for; matrix products, arithmetic and copies ran while one was open for 0% of the time, Pallas kernels for 0%

profile of v1, /device:TPU:0, one launch (start us, length us, event | category | flops | bytes accessed | tf_op | source)
XLA Modules:
  0.0 161.9 jit_solution(13113985034681718000)
XLA Ops:
  7.2 0.0 copy-start
  7.2 0.0 copy-start.1
  7.2 0.0 all-reduce.3.cloned.1.call-start
  7.2 1.1 bitcast_convert_fusion
  8.3 3.0 %collective-permute-start = (f32[16,13312]{1,0:T(8,128)S(1)}, f32[16,13312]{1,0:T(8,128)S(1)}, u32[]{:S(2)}, u32[]{:S(2)}) collective-permute-start(f32[16,13312]{1,0:T(8,128)S(1)} %bitcast_convert_fusion), channel_id=1, source_target_pairs={{0,16},{16,0},{1,17},{17,1},{2,18},{18,2},{3,19},{19,3},{4,20},{20... | collective-permute-start | bytes 2555912 | tf_op jit(solution)/shard_map/ppermute | solution.py:17
  11.4 18.9 %collective-permute-done = f32[16,13312]{1,0:T(8,128)S(1)} collective-permute-done((f32[16,13312]{1,0:T(8,128)S(1)}, f32[16,13312]{1,0:T(8,128)S(1)}, u32[]{:S(2)}, u32[]{:S(2)}) %collective-permute-start) | collective-permute-done | bytes 852000 | tf_op jit(solution)/shard_map/ppermute | solution.py:17
  30.3 0.0 copy-done.1
  30.3 1.0 fusion.4
  31.3 0.0 all-reduce.3.cloned.1.call-update
  31.4 0.0 copy-start.10
  31.4 0.6 copy-done.10
  32.0 0.6 dynamic-slice
  33.2 45.5 %all-reduce.3.cloned.1.call-done = f32[16,13312]{1,0:T(8,128)} async-done(((f32[16,13312]{1,0:T(8,128)}), f32[16,13312]{1,0:T(8,128)}) %all-reduce.3.cloned.1.call-update) | async-done | bytes 851984
  78.8 0.0 copy-start.6
  78.8 1.7 %multiply_reduce_fusion = f32[]{:T(128)} fusion(f32[16,13312]{1,0:T(8,128)} %all-reduce.3.cloned.1.call-done, u32[]{:T(128)S(6)} %multiply.4), kind=kLoop, calls=%fused_computation.16 | loop fusion | flops 106495 | bytes 213000 | tf_op jit(solution)/shard_map/reduce_sum | solution.py:28
  80.5 0.0 copy-done
  80.5 0.0 copy-start.3
  80.5 0.0 copy-start.4
  80.5 0.1 broadcast_bitcast_fusion.1
  80.6 31.7 %psum.7 = f32[]{:T(128)} all-reduce(f32[]{:T(128)} %multiply_reduce_fusion), channel_id=1, replica_groups=mesh['dp'=2,'fsdp'=4,'tensor'=4] {'fsdp','tensor'}, use_global_device_ids=true, to_apply=%region_2.0 | all-reduce | flops 1 | bytes 8 | tf_op jit(solution)/shard_map/psum | solution.py:28
  113.0 0.0 copy-start.8
  113.0 0.0 copy-done.6
  113.0 0.0 copy-done.3
  113.0 0.0 copy-done.4
  113.0 0.6 copy-done.8
  113.6 1.5 abs_bitcast_fusion
  115.1 0.1 bitcast_reduce_fusion
  115.3 0.0 copy-start.7
  115.3 0.1 broadcast_bitcast_fusion
  115.4 0.4 copy-done.7
  115.9 0.0 copy-start.5
  115.9 16.5 %pmax.15 = f32[13312]{0:T(1024)S(1)} all-reduce(f32[13312]{0:T(1024)S(1)} %get-tuple-element.11), channel_id=1, replica_groups=mesh['dp'=2,'fsdp'=4,'tensor'=4] {'fsdp'}, use_global_device_ids=true, to_apply=%region_7.0 | all-reduce | flops 13312 | bytes 106496 | tf_op jit(solution)/shard_map/pmax | solution.py:54
  132.3 0.0 copy-start.2
  132.3 5.8 %pmax.14 = f32[4]{0:T(128)S(1)} all-reduce(f32[4]{0:T(128)S(1)} %get-tuple-element.12), channel_id=1, replica_groups=mesh['dp'=2,'fsdp'=4,'tensor'=4] {'tensor'}, use_global_device_ids=true, to_apply=%region_5.0 | all-reduce | flops 4 | bytes 32 | tf_op jit(solution)/shard_map/pmax | solution.py:53
  138.1 0.0 copy-start.9
  138.1 0.5 copy-done.9
  138.6 0.0 copy-done.5
  138.6 1.0 fusion.7
  139.6 0.0 copy-done.2
  139.7 14.6 %all-gather = bf16[4,4,13312]{2,1,0:T(4,128)(2,1)S(1)} all-gather(bf16[1,4,13312]{2,1,0:T(4,128)(2,1)S(1)} %get-tuple-element.15), channel_id=1, replica_groups=mesh['dp'=2,'fsdp'=4,'tensor'=4] {'fsdp'}, dimensions={0}, use_global_device_ids=true | all-gather | bytes 532480 | tf_op jit(solution)/shard_map/all_gather | solution.py:43
  154.2 0.9 reshape.32
  (1 shorter events, 0.0 us)
Async XLA Ops:
  7.2 73.3 %copy-start = (f32[4,104]{1,0:T(4,128)S(1)}, f32[4,104]{1,0:T(4,128)}, u32[]{:S(2)}) copy-start(f32[4,104]{1,0:T(4,128)} %param.10) | copy-start | bytes 4996
  7.2 23.1 %copy-start.1 = (bf16[1,1,16,13312]{3,2,1,0:T(8,128)(2,1)S(1)}, bf16[1,1,16,13312]{3,2,1,0:T(8,128)(2,1)}, u32[]{:S(2)}) copy-start(bf16[1,1,16,13312]{3,2,1,0:T(8,128)(2,1)} %param.7) | copy-start | bytes 1277956
  7.2 71.6 %all-reduce.3.cloned.1.call-start = ((), (), s32[]{:S(2)}) async-start(), calls=%async_computation | async-start | bytes 1703936
  8.3 22.0 %collective-permute-start = (f32[16,13312]{1,0:T(8,128)S(1)}, f32[16,13312]{1,0:T(8,128)S(1)}, u32[]{:S(2)}, u32[]{:S(2)}) collective-permute-start(f32[16,13312]{1,0:T(8,128)S(1)} %bitcast_convert_fusion), channel_id=1, source_target_pairs={{0,16},{16,0},{1,17},{17,1},{2,18},{18,2},{3,19},{19,3},{4,20},{20... | collective-permute-start | bytes 2555912 | tf_op jit(solution)/shard_map/ppermute | solution.py:17
  31.4 0.7 copy-start.10
  78.8 34.2 %copy-start.6 = (f32[13312]{0:T(1024)S(1)}, f32[13312]{0:T(1024)}, u32[]{:S(2)}) copy-start(f32[13312]{0:T(1024)} %param.13) | copy-start | bytes 159748
  80.5 32.5 %copy-start.3 = (bf16[4,13312]{1,0:T(4,128)(2,1)S(1)}, bf16[4,13312]{1,0:T(4,128)(2,1)}, u32[]{:S(2)}) copy-start(bf16[4,13312]{1,0:T(4,128)(2,1)} %param.9) | copy-start | bytes 319492
  80.5 32.5 %copy-start.4 = (bf16[4,13312]{1,0:T(4,128)(2,1)S(1)}, bf16[4,13312]{1,0:T(4,128)(2,1)}, u32[]{:S(2)}) copy-start(bf16[4,13312]{1,0:T(4,128)(2,1)} %param.11) | copy-start | bytes 319492
  113.0 0.7 copy-start.8
  115.3 0.6 copy-start.7
  115.9 22.8 %copy-start.5 = (bf16[4,13312]{1,0:T(4,128)(2,1)S(1)}, bf16[4,13312]{1,0:T(4,128)(2,1)}, u32[]{:S(2)}) copy-start(bf16[4,13312]{1,0:T(4,128)(2,1)} %param.8) | copy-start | bytes 319492
  132.3 7.3 %copy-start.2 = (f32[13312]{0:T(1024)}, f32[13312]{0:T(1024)S(1)}, u32[]{:S(2)}) copy-start(f32[13312]{0:T(1024)S(1)} %pmax.15) | copy-start | bytes 159748
  138.1 0.5 copy-start.9
Sparse Core Ops, SparseCore 0:
  31.5 47.2 all-reduce.2
